TPU v7x, 32 devices: a whole 2x2x4 slice. The times are simulated.
32 devices in a mesh: iface: 8 (over z, y), dom: 4 (over x, core).
Axes of the slice: x: 2, y: 2, z: 4, core: 2. Of those that a mesh axis runs over, the one named last changes fastest.
Arguments:
- interface: float32 [131072], P(('iface', 'dom')), may hold values from -6 to 6
- previous_residual: float32 [131072], P(('iface', 'dom')), may hold values from -6 to 6
- previous_estimate: float32 [131072], P(('iface', 'dom')), may hold values from -6 to 6
- forcing: float32 [131072], P(('iface', 'dom')), may hold values from -60 to 60
- stiffness: float32 [131072], P(('iface', 'dom')), may hold values from 0.2 to 0.6
- history_residual: float32 [100, 131072], P(None, ('iface', 'dom')), may hold values from -40 to 40
- history_estimate: float32 [100, 131072], P(None, ('iface', 'dom')), may hold values from -6 to 6
Outputs:
- interface_next: float32 [131072], P(('iface', 'dom'))
- residual_last: float32 [131072], P(('iface', 'dom'))
All inputs are finite; a program needn't handle non-finite values.
Results may differ from a plain program's by a relative error of at most 0.0003.
Values sent between devices are 32-bit elements; how exact they have to be, the bound alone decides.
A program may use at most 64 MiB of HBM per device.

v0:
```python
import jax
import jax.numpy as jnp
from jax import lax
from jax.sharding import PartitionSpec as P

ITERS = 3
coupling = 0.25


def from_behind(value, axis, steps):
    count = lax.axis_size(axis)
    initial, last = (max(0, -steps), min(count, count - steps))
    return lax.ppermute(value, axis, [(source, source + steps) for source in range(initial, last)])


def solver_map(current, forcing, stiffness):
    from_left = from_behind(current[-1:], ("iface", "dom"), 1)
    from_right = from_behind(current[:1], ("iface", "dom"), -1)
    padded = jnp.concatenate([from_left, current, from_right], axis=0)
    return forcing + stiffness * jnp.tanh(current) + coupling * (padded[:-2] + padded[2:])


def shards(
    interface,
    previous_residual,
    previous_estimate,
    forcing,
    stiffness,
    history_residual,
    history_estimate,
):
    high = lax.Precision.HIGHEST
    current = interface
    hist_v = history_residual
    hist_w = history_estimate
    old_residual = previous_residual
    old_estimate = previous_estimate
    residual = previous_residual
    for iteration in range(ITERS):
        estimate = solver_map(current, forcing, stiffness)
        residual = estimate - current
        new_column = residual - old_residual
        hist_v = jnp.concatenate([hist_v, new_column[None, :]], axis=0)
        hist_w = jnp.concatenate([hist_w, (estimate - old_estimate)[None, :]], axis=0)
        gram_matrix, projection = lax.psum(
            (jnp.dot(hist_v, hist_v.T, precision=high), jnp.dot(hist_v, residual, precision=high)),
            ("iface", "dom"),
        )
        factor = jnp.linalg.cholesky(gram_matrix)
        coeffs = -jax.scipy.linalg.cho_solve((factor, True), projection)
        current = estimate + jnp.dot(coeffs, hist_w, precision=high)
        old_residual = residual
        old_estimate = estimate
    return (current, residual)


def solution(mesh):
    return jax.shard_map(
        shards,
        mesh=mesh,
        in_specs=(
            P(("iface", "dom")),
            P(("iface", "dom")),
            P(("iface", "dom")),
            P(("iface", "dom")),
            P(("iface", "dom")),
            P(None, ("iface", "dom")),
            P(None, ("iface", "dom")),
        ),
        out_specs=(P(("iface", "dom")), P(("iface", "dom"))),
        check_vma=False,
    )
```

profile of v0, /device:TPU:0, one launch (start us, length us, event | category | flops | bytes accessed | tf_op | source)
XLA Modules:
  0.0 240.4 jit_solution(12346703330274250481)
XLA Ops:
  0.6 1.4 fusion.75
  2.1 2.9 %collective-permute-start = (f32[1]{0:T(128)}, f32[1]{0:T(128)}, u32[]{:S(2)}, u32[]{:S(2)}) collective-permute-start(f32[1]{0:T(128)} %get-tuple-element.24), channel_id=1, source_target_pairs={{0,1},{1,2},{2,3},{3,4},{4,5},{5,6},{6,7},{7,8},{8,9},{9,10},{10,1... | collective-permute-start | bytes 20 | tf_op jit(solution)/shard_map/ppermute | solution.py:13
  5.0 1.3 collective-permute-start.1
  6.3 3.4 %collective-permute-done.1 = f32[1]{0:T(128)} collective-permute-done((f32[1]{0:T(128)}, f32[1]{0:T(128)}, u32[]{:S(2)}, u32[]{:S(2)}) %collective-permute-start.1) | collective-permute-done | bytes 36 | tf_op jit(solution)/shard_map/ppermute | solution.py:13
  9.7 2.8 %fusion.70 = (f32[4096]{0:T(1024)}, f32[4096]{0:T(1024)S(1)}) fusion(f32[4096]{0:T(1024)} %param.9, f32[1]{0:T(128)} %collective-permute-done.1, f32[4096]{0:T(1024)} %param.7, f32[1]{0:T(128)} %collective-permute-done, f32[4096]{0:T(1024)} %param.10, f32[4096]{0:T(1024)} %param.11), kind=kLoop, calls=%fused_computation.102 | loop fusion | flops 32768 | bytes 98312 | tf_op jit(solution)/shard_map/sub | solution.py:44
  12.5 0.7 fusion.72
  13.3 3.6 %fusion.19 = f32[101,101]{0,1:T(8,128)S(1)} fusion(f32[1,4096]{1,0:T(1,128)S(1)} %bitcast.102, f32[100,4096]{1,0:T(8,128)} %param.12), kind=kOutput, calls=%fused_computation.22 | convolution fusion | flops 501813248 | bytes 1695588 | tf_op jit(solution)/shard_map/dot_general | solution.py:46
  17.0 1.4 fusion.29
  18.4 43.2 %all-reduce.2 = (f32[101,101]{0,1:T(8,128)S(1)}, f32[101]{0:T(128)S(1)}) all-reduce(f32[101,101]{0,1:T(8,128)S(1)} %fusion.19, f32[101]{0:T(128)S(1)} %fusion.29), channel_id=1, replica_groups=mesh['iface'=8,'dom'=4] {'iface','dom'}, use_global_device_ids=true, to_apply=%region_0.0 | all-reduce | flops 10302 | bytes 82416 | tf_op jit(solution)/shard_map/psum | solution.py:45
  61.7 0.6 fusion.42
  62.4 10.1 %cholesky.44 = f32[101,101]{1,0:T(8,128)S(1)} custom-call(f32[101,101]{1,0:T(8,128)} %fusion.42), custom_call_target="Cholesky" | custom-call | tf_op jit(solution)/shard_map/jit(cholesky)/cholesky | solution.py:49
  72.5 0.7 compare_reduce_fusion.2
  73.2 1.3 fusion.31
  74.5 8.5 %custom-call.30 = f32[1,101,101]{1,2,0:T(8,128)S(1)} custom-call(f32[1,101,101]{2,1,0:T(8,128)} %fusion.31), custom_call_target="InvertDiagBlocksLowerTriangular" | custom-call | tf_op jit(solution)/shard_map/jit(_cho_solve)/triangular_solve | solution.py:50
  83.1 0.2 convolution_bitcast_fusion.6
  83.2 0.2 fusion.23
  83.4 1.7 fusion
  85.1 0.7 fusion.74
  85.8 1.9 collective-permute-start.2
  87.6 1.5 collective-permute-start.3
  89.1 3.7 %collective-permute-done.3 = f32[1]{0:T(128)} collective-permute-done((f32[1]{0:T(128)}, f32[1]{0:T(128)}, u32[]{:S(2)}, u32[]{:S(2)}) %collective-permute-start.3) | collective-permute-done | bytes 36 | tf_op jit(solution)/shard_map/ppermute | solution.py:13
  92.8 1.9 fusion.67
  94.7 2.1 fusion.21
  96.9 1.4 fusion.28
  98.3 42.2 %all-reduce.1 = (f32[102,102]{0,1:T(8,128)S(1)}, f32[102]{0:T(128)S(1)}) all-reduce(f32[102,102]{0,1:T(8,128)} %fusion.21, f32[102]{0:T(128)S(1)} %fusion.28), channel_id=1, replica_groups=mesh['iface'=8,'dom'=4] {'iface','dom'}, use_global_device_ids=true, to_apply=%region_4.5 | all-reduce | flops 10506 | bytes 84048 | tf_op jit(solution)/shard_map/psum | solution.py:45
  140.6 0.6 fusion.39
  141.3 10.2 %cholesky.86 = f32[102,102]{1,0:T(8,128)S(1)} custom-call(f32[102,102]{1,0:T(8,128)} %fusion.39), custom_call_target="Cholesky" | custom-call | tf_op jit(solution)/shard_map/jit(cholesky)/cholesky | solution.py:49
  151.5 0.7 compare_reduce_fusion.1
  152.1 1.3 fusion.32
  153.4 8.6 %custom-call.31 = f32[1,102,102]{1,2,0:T(8,128)S(1)} custom-call(f32[1,102,102]{2,1,0:T(8,128)} %fusion.32), custom_call_target="InvertDiagBlocksLowerTriangular" | custom-call | tf_op jit(solution)/shard_map/jit(_cho_solve)/triangular_solve | solution.py:50
  162.1 0.2 convolution_bitcast_fusion.4
  162.2 0.2 fusion.25
  162.4 1.7 fusion.4
  164.1 0.6 fusion.73
  164.7 1.8 collective-permute-start.4
  166.6 1.3 collective-permute-start.5
  167.9 3.9 %collective-permute-done.5 = f32[1]{0:T(128)} collective-permute-done((f32[1]{0:T(128)}, f32[1]{0:T(128)}, u32[]{:S(2)}, u32[]{:S(2)}) %collective-permute-start.5) | collective-permute-done | bytes 36 | tf_op jit(solution)/shard_map/ppermute | solution.py:13
  171.8 1.9 fusion.64
  173.7 1.5 fusion.30
  175.3 1.4 convolution_bitcast_fusion.2
  176.7 42.2 %all-reduce = (f32[103,103]{0,1:T(8,128)S(1)}, f32[103]{0:T(128)S(1)}) all-reduce(f32[103,103]{0,1:T(8,128)S(1)} %fusion.30, f32[103]{0:T(128)S(1)} %convolution_bitcast_fusion.2), channel_id=1, replica_groups=mesh['iface'=8,'dom'=4] {'iface','dom'}, use_global_device_ids=true, to_apply=%region_8.9 | all-reduce | flops 10712 | bytes 85696 | tf_op jit(solution)/shard_map/psum | solution.py:45
  219.0 9.4 %cholesky.96 = f32[103,103]{1,0:T(8,128)S(1)} custom-call(f32[103,103]{1,0:T(8,128)S(1)} %fusion.36), custom_call_target="Cholesky" | custom-call | tf_op jit(solution)/shard_map/jit(cholesky)/cholesky | solution.py:49
  228.4 0.7 compare_reduce_fusion
  229.1 0.6 fusion.33
  229.8 7.9 %custom-call.32 = f32[1,103,103]{1,2,0:T(8,128)S(1)} custom-call(f32[1,103,103]{2,1,0:T(8,128)S(1)} %fusion.33), custom_call_target="InvertDiagBlocksLowerTriangular" | custom-call | tf_op jit(solution)/shard_map/jit(_cho_solve)/triangular_solve | solution.py:50
  237.8 0.2 fusion.27
  238.1 1.7 fusion.10
  239.8 0.6 add.107
  (49 shorter events, 0.7 us)
Async XLA Ops:
  0.6 16.3 %copy-start = (f32[100,4096]{1,0:T(8,128)S(1)}, f32[100,4096]{1,0:T(8,128)}, u32[]{:S(2)}) copy-start(f32[100,4096]{1,0:T(8,128)} %param.12) | copy-start | bytes 4915204
  2.1 4.2 %collective-permute-start = (f32[1]{0:T(128)}, f32[1]{0:T(128)}, u32[]{:S(2)}, u32[]{:S(2)}) collective-permute-start(f32[1]{0:T(128)} %get-tuple-element.24), channel_id=1, source_target_pairs={{0,1},{1,2},{2,3},{3,4},{4,5},{5,6},{6,7},{7,8},{8,9},{9,10},{10,1... | collective-permute-start | bytes 20 | tf_op jit(solution)/shard_map/ppermute | solution.py:13
  5.0 4.7 %collective-permute-start.1 = (f32[1]{0:T(128)}, f32[1]{0:T(128)}, u32[]{:S(2)}, u32[]{:S(2)}) collective-permute-start(f32[1]{0:T(128)} %get-tuple-element.25), channel_id=1, source_target_pairs={{1,0},{2,1},{3,2},{4,3},{5,4},{6,5},{7,6},{8,7},{9,8},{10,9},{11,1... | collective-permute-start | bytes 20 | tf_op jit(solution)/shard_map/ppermute | solution.py:13
  13.3 3.7 %copy-start.4 = (f32[4096]{0:T(1024)}, f32[4096]{0:T(1024)S(1)}, u32[]{:S(2)}) copy-start(f32[4096]{0:T(1024)S(1)} %get-tuple-element.19) | copy-start | bytes 49156
  13.3 5.1 %copy-start.2 = (f32[4096]{0:T(1024)}, f32[4096]{0:T(1024)S(1)}, u32[]{:S(2)}) copy-start(f32[4096]{0:T(1024)S(1)} %get-tuple-element.18) | copy-start | bytes 49156
  13.3 70.1 %copy-start.1 = (f32[100,4096]{1,0:T(8,128)S(1)}, f32[100,4096]{1,0:T(8,128)}, u32[]{:S(2)}) copy-start(f32[100,4096]{1,0:T(8,128)} %param.13) | copy-start | bytes 4915204
  62.4 30.4 %copy-start.6 = (f32[4096]{0:T(1024)S(1)}, f32[4096]{0:T(1024)}, u32[]{:S(2)}) copy-start(f32[4096]{0:T(1024)} %param.10) | copy-start | bytes 49156
  62.4 32.3 %copy-start.5 = (f32[4096]{0:T(1024)S(1)}, f32[4096]{0:T(1024)}, u32[]{:S(2)}) copy-start(f32[4096]{0:T(1024)} %copy-done.4) | copy-start | bytes 49156
  62.4 32.4 %copy-start.3 = (f32[4096]{0:T(1024)S(1)}, f32[4096]{0:T(1024)}, u32[]{:S(2)}) copy-start(f32[4096]{0:T(1024)} %copy-done.2) | copy-start | bytes 49156
  83.1 9.7 %copy-start.8 = (f32[4096]{0:T(1024)S(1)}, f32[4096]{0:T(1024)}, u32[]{:S(2)}) copy-start(f32[4096]{0:T(1024)} %param.11) | copy-start | bytes 49156
  85.8 3.3 %collective-permute-start.2 = (f32[1]{0:T(128)}, f32[1]{0:T(128)}, u32[]{:S(2)}, u32[]{:S(2)}) collective-permute-start(f32[1]{0:T(128)} %get-tuple-element.22), channel_id=1, source_target_pairs={{0,1},{1,2},{2,3},{3,4},{4,5},{5,6},{6,7},{7,8},{8,9},{9,10},{10,1... | collective-permute-start | bytes 20 | tf_op jit(solution)/shard_map/ppermute | solution.py:13
  87.6 5.2 %collective-permute-start.3 = (f32[1]{0:T(128)}, f32[1]{0:T(128)}, u32[]{:S(2)}, u32[]{:S(2)}) collective-permute-start(f32[1]{0:T(128)} %get-tuple-element.23), channel_id=1, source_target_pairs={{1,0},{2,1},{3,2},{4,3},{5,4},{6,5},{7,6},{8,7},{9,8},{10,9},{11,1... | collective-permute-start | bytes 20 | tf_op jit(solution)/shard_map/ppermute | solution.py:13
  94.7 2.1 copy-start.14
  94.7 3.6 %copy-start.11 = (f32[4096]{0:T(1024)}, f32[4096]{0:T(1024)S(1)}, u32[]{:S(2)}) copy-start(f32[4096]{0:T(1024)S(1)} %get-tuple-element.15) | copy-start | bytes 49156
  141.3 30.5 %copy-start.7 = (f32[4096]{0:T(1024)S(1)}, f32[4096]{0:T(1024)}, u32[]{:S(2)}) copy-start(f32[4096]{0:T(1024)} %param.10) | copy-start | bytes 49156
  141.3 30.5 %copy-start.9 = (f32[4096]{0:T(1024)S(1)}, f32[4096]{0:T(1024)}, u32[]{:S(2)}) copy-start(f32[4096]{0:T(1024)} %param.11) | copy-start | bytes 49156
  162.0 11.7 %copy-start.12 = (f32[4096]{0:T(1024)S(1)}, f32[4096]{0:T(1024)}, u32[]{:S(2)}) copy-start(f32[4096]{0:T(1024)} %copy-done.11) | copy-start | bytes 49156
  162.0 11.7 %copy-start.15 = (f32[4096]{0:T(1024)S(1)}, f32[4096]{0:T(1024)}, u32[]{:S(2)}) copy-start(f32[4096]{0:T(1024)} %copy-done.14) | copy-start | bytes 49156
  164.7 3.1 %collective-permute-start.4 = (f32[1]{0:T(128)}, f32[1]{0:T(128)}, u32[]{:S(2)}, u32[]{:S(2)}) collective-permute-start(f32[1]{0:T(128)} %get-tuple-element.20), channel_id=1, source_target_pairs={{0,1},{1,2},{2,3},{3,4},{4,5},{5,6},{6,7},{7,8},{8,9},{9,10},{10,1... | collective-permute-start | bytes 20 | tf_op jit(solution)/shard_map/ppermute | solution.py:13
  166.6 5.2 %collective-permute-start.5 = (f32[1]{0:T(128)}, f32[1]{0:T(128)}, u32[]{:S(2)}, u32[]{:S(2)}) collective-permute-start(f32[1]{0:T(128)} %get-tuple-element.21), channel_id=1, source_target_pairs={{1,0},{2,1},{3,2},{4,3},{5,4},{6,5},{7,6},{8,7},{9,8},{10,9},{11,1... | collective-permute-start | bytes 20 | tf_op jit(solution)/shard_map/ppermute | solution.py:13
  173.7 3.0 %copy-start.16 = (f32[4096]{0:T(1024)}, f32[4096]{0:T(1024)S(1)}, u32[]{:S(2)}) copy-start(f32[4096]{0:T(1024)S(1)} %get-tuple-element.11) | copy-start | bytes 49156
  175.2 62.8 %copy-start.10 = (f32[4096]{0:T(1024)S(1)}, f32[4096]{0:T(1024)}, u32[]{:S(2)}) copy-start(f32[4096]{0:T(1024)} %get-tuple-element.16) | copy-start | bytes 49156
  175.3 62.8 %copy-start.13 = (f32[4096]{0:T(1024)S(1)}, f32[4096]{0:T(1024)}, u32[]{:S(2)}) copy-start(f32[4096]{0:T(1024)} %get-tuple-element.12) | copy-start | bytes 49156
where the time goes:
time: 242 us; the launch traced here: 240 us
  blocking collectives  128 us (53%)
  other arithmetic  69.4 us (29%)
  matrix products  17.6 us (7%)
  waiting for transfers between devices  11 us (5%)
  starting transfers between devices  10.6 us (4%)
  local copies, waits for them, and re-layouts  3.08 us (1%)
    psum x3, blocking collectives, shards(): lax.psum((jnp.dot(hist_v, hist_v.T, precision=high), jnp.dot(hist_v, resi...  128 us
    another operation x9, other arithmetic, shards(): factor = jnp.linalg.cholesky(gram_matrix)  31.8 us
    another operation x6, other arithmetic, shards(): coeffs = -jax.scipy.linalg.cho_solve((factor, True), projection)  28.3 us
    ppermute x6, waiting for transfers between devices, from_behind(): lax.ppermute(value, axis, [(source, source + steps) for source in range(i...  11 us
    ppermute x6, starting transfers between devices, from_behind(): lax.ppermute(value, axis, [(source, source + steps) for source in range(i...  10.6 us
    dot_general x3, matrix products, shards(): jnp.dot(hist_v, hist_v.T, precision=high)  7.23 us
    sub x3, other arithmetic, shards(): estimate - old_estimate  6.7 us
    dot_general x3, matrix products, shards(): current = estimate + jnp.dot(coeffs, hist_w, precision=high)  5.13 us
  transfers between devices with their start and end apart: 6, of which 3 were waited for; matrix products, arithmetic and copies ran while one was open for 0% of the time, Pallas kernels for 0%

commit v1 on v0

--- a/solution.py
+++ b/solution.py
@@ -43,8 +43,14 @@
         hist_v = jnp.concatenate([hist_v, new_column[None, :]], axis=0)
         hist_w = jnp.concatenate([hist_w, (estimate - old_estimate)[None, :]], axis=0)
         gram_matrix, projection = lax.psum(
-            (jnp.dot(hist_v, hist_v.T, precision=high), jnp.dot(hist_v, residual, precision=high)),
-            ("iface", "dom"),
+            lax.psum(
+                (
+                    jnp.dot(hist_v, hist_v.T, precision=high),
+                    jnp.dot(hist_v, residual, precision=high),
+                ),
+                "dom",
+            ),
+            "iface",
         )
         factor = jnp.linalg.cholesky(gram_matrix)
         coeffs = -jax.scipy.linalg.cho_solve((factor, True), projection)

time: 242 us -> 261 us (1.079)
  blocking collectives: 128 us -> 149 us
    psum x0 -> x3, blocking collectives: none -> 108 us  [shards(): lax.psum(lax.psum((jnp.dot(hist_v, hist_v.T, precision=high), jnp.dot(his...]
    psum x3, blocking collectives: 128 us -> 41.2 us  [shards(): lax.psum((jnp.dot(hist_v, hist_v.T, precision=high), jnp.dot(hist_v, resi...]
where the time goes in v1:
time: 261 us; the launch traced here: 259 us
  blocking collectives  149 us (57%)
  other arithmetic  69.9 us (27%)
  matrix products  17 us (7%)
  starting transfers between devices  10.4 us (4%)
  waiting for transfers between devices  8.95 us (3%)
  local copies, waits for them, and re-layouts  3.04 us (1%)
    psum x3, blocking collectives, shards(): lax.psum(lax.psum((jnp.dot(hist_v, hist_v.T, precision=high), jnp.dot(his...  108 us
    psum x3, blocking collectives, shards(): lax.psum((jnp.dot(hist_v, hist_v.T, precision=high), jnp.dot(hist_v, resi...  41.2 us
    another operation x9, other arithmetic, shards(): factor = jnp.linalg.cholesky(gram_matrix)  31.7 us
    another operation x6, other arithmetic, shards(): coeffs = -jax.scipy.linalg.cho_solve((factor, True), projection)  28.2 us
    ppermute x6, starting transfers between devices, from_behind(): lax.ppermute(value, axis, [(source, source + steps) for source in range(i...  10.4 us
    ppermute x6, waiting for transfers between devices, from_behind(): lax.ppermute(value, axis, [(source, source + steps) for source in range(i...  8.95 us
    sub x3, other arithmetic, shards(): estimate - old_estimate  7.28 us
    dot_general x3, matrix products, shards(): jnp.dot(hist_v, hist_v.T, precision=high)  6.62 us
  transfers between devices with their start and end apart: 6, of which 3 were waited for; matrix products, arithmetic and copies ran while one was open for 0% of the time, Pallas kernels for 0%

profile of v1, /device:TPU:0, one launch (start us, length us, event | category | flops | bytes accessed | tf_op | source)
XLA Modules:
  0.0 259.1 jit_solution(5965126121899318292)
XLA Ops:
  0.6 1.4 fusion.75
  2.1 2.9 %collective-permute-start = (f32[1]{0:T(128)}, f32[1]{0:T(128)}, u32[]{:S(2)}, u32[]{:S(2)}) collective-permute-start(f32[1]{0:T(128)} %get-tuple-element.30), channel_id=1, source_target_pairs={{0,1},{1,2},{2,3},{3,4},{4,5},{5,6},{6,7},{7,8},{8,9},{9,10},{10,1... | collective-permute-start | bytes 20 | tf_op jit(solution)/shard_map/ppermute | solution.py:13
  5.0 1.3 collective-permute-start.1
  6.3 3.6 %collective-permute-done.1 = f32[1]{0:T(128)} collective-permute-done((f32[1]{0:T(128)}, f32[1]{0:T(128)}, u32[]{:S(2)}, u32[]{:S(2)}) %collective-permute-start.1) | collective-permute-done | bytes 36 | tf_op jit(solution)/shard_map/ppermute | solution.py:13
  9.9 2.7 %fusion.70 = (f32[4096]{0:T(1024)}, f32[4096]{0:T(1024)S(1)}) fusion(f32[4096]{0:T(1024)} %param.9, f32[1]{0:T(128)} %collective-permute-done.1, f32[4096]{0:T(1024)} %param.7, f32[1]{0:T(128)} %collective-permute-done, f32[4096]{0:T(1024)} %param.10, f32[4096]{0:T(1024)} %param.11), kind=kLoop, calls=%fused_computation.102 | loop fusion | flops 32768 | bytes 98312 | tf_op jit(solution)/shard_map/sub | solution.py:44
  12.6 0.7 fusion.72
  13.3 3.6 %fusion.19 = f32[101,101]{0,1:T(8,128)S(1)} fusion(f32[1,4096]{1,0:T(1,128)S(1)} %bitcast.102, f32[100,4096]{1,0:T(8,128)} %param.12), kind=kOutput, calls=%fused_computation.22 | convolution fusion | flops 501813248 | bytes 1695588 | tf_op jit(solution)/shard_map/dot_general | solution.py:48
  17.0 1.4 fusion.29
  18.4 14.8 %all-reduce.5 = (f32[101,101]{0,1:T(8,128)S(1)}, f32[101]{0:T(128)S(1)}) all-reduce(f32[101,101]{0,1:T(8,128)S(1)} %fusion.19, f32[101]{0:T(128)S(1)} %fusion.29), channel_id=1, replica_groups=mesh['iface'=8,'dom'=4] {'dom'}, use_global_device_ids=true, to_apply=%region_0.0 | all-reduce | flops 10302 | bytes 82416 | tf_op jit(solution)/shard_map/psum | solution.py:46
  33.2 36.0 %all-reduce.2 = (f32[101,101]{0,1:T(8,128)S(1)}, f32[101]{0:T(128)S(1)}) all-reduce(f32[101,101]{0,1:T(8,128)S(1)} %get-tuple-element.12, f32[101]{0:T(128)S(1)} %get-tuple-element.13), channel_id=1, replica_groups=mesh['iface'=8,'dom'=4] {'iface'}, use_global_device_ids=true, to_apply=%region_1.0 | all-reduce | flops 10302 | bytes 82416 | tf_op jit(solution)/shard_map/psum | solution.py:45
  69.3 0.6 fusion.42
  70.0 10.1 %cholesky.44 = f32[101,101]{1,0:T(8,128)S(1)} custom-call(f32[101,101]{1,0:T(8,128)} %fusion.42), custom_call_target="Cholesky" | custom-call | tf_op jit(solution)/shard_map/jit(cholesky)/cholesky | solution.py:55
  80.1 0.6 compare_reduce_fusion.2
  80.7 1.2 fusion.31
  81.9 8.5 %custom-call.30 = f32[1,101,101]{1,2,0:T(8,128)S(1)} custom-call(f32[1,101,101]{2,1,0:T(8,128)} %fusion.31), custom_call_target="InvertDiagBlocksLowerTriangular" | custom-call | tf_op jit(solution)/shard_map/jit(_cho_solve)/triangular_solve | solution.py:56
  90.6 0.2 fusion.23
  90.8 1.7 fusion
  92.5 0.6 fusion.74
  93.1 1.8 collective-permute-start.2
  94.9 1.3 collective-permute-start.3
  96.2 3.3 %collective-permute-done.3 = f32[1]{0:T(128)} collective-permute-done((f32[1]{0:T(128)}, f32[1]{0:T(128)}, u32[]{:S(2)}, u32[]{:S(2)}) %collective-permute-start.3) | collective-permute-done | bytes 36 | tf_op jit(solution)/shard_map/ppermute | solution.py:13
  99.5 2.7 %fusion.67 = (f32[4096]{0:T(1024)}, f32[4096]{0:T(1024)S(1)}) fusion(f32[4096]{0:T(1024)S(1)} %get-tuple-element.23, f32[1]{0:T(128)} %collective-permute-done.3, f32[4096]{0:T(1024)S(1)} %add.109, f32[1]{0:T(128)} %collective-permute-done.2, f32[4096]{0:T(1024)} %param.10, f32[4096]{0:T(1024)} %param.11), kind=kLoop, calls=%fused_computation.100 | loop fusion | flops 32768 | bytes 98312 | tf_op jit(solution)/shard_map/sub | solution.py:44
  102.2 1.5 fusion.21
  103.7 1.4 fusion.28
  105.1 13.3 %all-reduce.4 = (f32[102,102]{0,1:T(8,128)}, f32[102]{0:T(128)S(1)}) all-reduce(f32[102,102]{0,1:T(8,128)S(1)} %fusion.21, f32[102]{0:T(128)S(1)} %fusion.28), channel_id=1, replica_groups=mesh['iface'=8,'dom'=4] {'dom'}, use_global_device_ids=true, to_apply=%region_6.7 | all-reduce | flops 10506 | bytes 84048 | tf_op jit(solution)/shard_map/psum | solution.py:46
  118.4 35.6 %all-reduce.1 = (f32[102,102]{0,1:T(8,128)S(1)}, f32[102]{0:T(128)S(1)}) all-reduce(f32[102,102]{0,1:T(8,128)} %get-tuple-element.10, f32[102]{0:T(128)S(1)} %get-tuple-element.11), channel_id=1, replica_groups=mesh['iface'=8,'dom'=4] {'iface'}, use_global_device_ids=true, to_apply=%region_7.8 | all-reduce | flops 10506 | bytes 84048 | tf_op jit(solution)/shard_map/psum | solution.py:45
  154.1 0.6 fusion.39
  154.7 10.2 %cholesky.86 = f32[102,102]{1,0:T(8,128)S(1)} custom-call(f32[102,102]{1,0:T(8,128)} %fusion.39), custom_call_target="Cholesky" | custom-call | tf_op jit(solution)/shard_map/jit(cholesky)/cholesky | solution.py:55
  164.9 0.7 compare_reduce_fusion.1
  165.6 1.3 fusion.32
  167.0 8.6 %custom-call.31 = f32[1,102,102]{1,2,0:T(8,128)S(1)} custom-call(f32[1,102,102]{2,1,0:T(8,128)} %fusion.32), custom_call_target="InvertDiagBlocksLowerTriangular" | custom-call | tf_op jit(solution)/shard_map/jit(_cho_solve)/triangular_solve | solution.py:56
  175.9 1.7 fusion.4
  177.7 0.7 fusion.73
  178.3 1.8 collective-permute-start.4
  180.1 1.3 collective-permute-start.5
  181.4 2.1 collective-permute-done.5
  183.5 1.9 fusion.64
  185.5 1.5 fusion.30
  187.0 1.4 convolution_bitcast_fusion.2
  188.4 13.1 %all-reduce.3 = (f32[103,103]{0,1:T(8,128)S(1)}, f32[103]{0:T(128)S(1)}) all-reduce(f32[103,103]{0,1:T(8,128)S(1)} %fusion.30, f32[103]{0:T(128)S(1)} %convolution_bitcast_fusion.2), channel_id=1, replica_groups=mesh['iface'=8,'dom'=4] {'dom'}, use_global_device_ids=true, to_apply=%region_12.13 | all-reduce | flops 10712 | bytes 85696 | tf_op jit(solution)/shard_map/psum | solution.py:46
  201.5 36.1 %all-reduce = (f32[103,103]{0,1:T(8,128)S(1)}, f32[103]{0:T(128)S(1)}) all-reduce(f32[103,103]{0,1:T(8,128)S(1)} %get-tuple-element.8, f32[103]{0:T(128)S(1)} %get-tuple-element.9), channel_id=1, replica_groups=mesh['iface'=8,'dom'=4] {'iface'}, use_global_device_ids=true, to_apply=%region_13.14 | all-reduce | flops 10712 | bytes 85696 | tf_op jit(solution)/shard_map/psum | solution.py:45
  237.7 9.4 %cholesky.96 = f32[103,103]{1,0:T(8,128)S(1)} custom-call(f32[103,103]{1,0:T(8,128)S(1)} %fusion.36), custom_call_target="Cholesky" | custom-call | tf_op jit(solution)/shard_map/jit(cholesky)/cholesky | solution.py:55
  247.2 0.7 compare_reduce_fusion
  247.9 0.6 fusion.33
  248.5 7.9 %custom-call.32 = f32[1,103,103]{1,2,0:T(8,128)S(1)} custom-call(f32[1,103,103]{2,1,0:T(8,128)S(1)} %fusion.33), custom_call_target="InvertDiagBlocksLowerTriangular" | custom-call | tf_op jit(solution)/shard_map/jit(_cho_solve)/triangular_solve | solution.py:56
  256.6 0.2 fusion.27
  256.8 1.7 fusion.10
  258.5 0.6 add.119
  (48 shorter events, 1.2 us)
Async XLA Ops:
  0.6 16.4 %copy-start = (f32[100,4096]{1,0:T(8,128)S(1)}, f32[100,4096]{1,0:T(8,128)}, u32[]{:S(2)}) copy-start(f32[100,4096]{1,0:T(8,128)} %param.12) | copy-start | bytes 4915204
  2.1 4.2 %collective-permute-start = (f32[1]{0:T(128)}, f32[1]{0:T(128)}, u32[]{:S(2)}, u32[]{:S(2)}) collective-permute-start(f32[1]{0:T(128)} %get-tuple-element.30), channel_id=1, source_target_pairs={{0,1},{1,2},{2,3},{3,4},{4,5},{5,6},{6,7},{7,8},{8,9},{9,10},{10,1... | collective-permute-start | bytes 20 | tf_op jit(solution)/shard_map/ppermute | solution.py:13
  5.0 4.9 %collective-permute-start.1 = (f32[1]{0:T(128)}, f32[1]{0:T(128)}, u32[]{:S(2)}, u32[]{:S(2)}) collective-permute-start(f32[1]{0:T(128)} %get-tuple-element.31), channel_id=1, source_target_pairs={{1,0},{2,1},{3,2},{4,3},{5,4},{6,5},{7,6},{8,7},{9,8},{10,9},{11,1... | collective-permute-start | bytes 20 | tf_op jit(solution)/shard_map/ppermute | solution.py:13
  13.3 3.7 %copy-start.4 = (f32[4096]{0:T(1024)}, f32[4096]{0:T(1024)S(1)}, u32[]{:S(2)}) copy-start(f32[4096]{0:T(1024)S(1)} %get-tuple-element.25) | copy-start | bytes 49156
  13.3 5.1 %copy-start.2 = (f32[4096]{0:T(1024)}, f32[4096]{0:T(1024)S(1)}, u32[]{:S(2)}) copy-start(f32[4096]{0:T(1024)S(1)} %get-tuple-element.24) | copy-start | bytes 49156
  13.3 77.5 %copy-start.1 = (f32[100,4096]{1,0:T(8,128)S(1)}, f32[100,4096]{1,0:T(8,128)}, u32[]{:S(2)}) copy-start(f32[100,4096]{1,0:T(8,128)} %param.13) | copy-start | bytes 4915204
  70.0 32.1 %copy-start.5 = (f32[4096]{0:T(1024)S(1)}, f32[4096]{0:T(1024)}, u32[]{:S(2)}) copy-start(f32[4096]{0:T(1024)} %copy-done.4) | copy-start | bytes 49156
  70.0 32.2 %copy-start.3 = (f32[4096]{0:T(1024)S(1)}, f32[4096]{0:T(1024)}, u32[]{:S(2)}) copy-start(f32[4096]{0:T(1024)} %copy-done.2) | copy-start | bytes 49156
  93.1 3.1 %collective-permute-start.2 = (f32[1]{0:T(128)}, f32[1]{0:T(128)}, u32[]{:S(2)}, u32[]{:S(2)}) collective-permute-start(f32[1]{0:T(128)} %get-tuple-element.28), channel_id=1, source_target_pairs={{0,1},{1,2},{2,3},{3,4},{4,5},{5,6},{6,7},{7,8},{8,9},{9,10},{10,1... | collective-permute-start | bytes 20 | tf_op jit(solution)/shard_map/ppermute | solution.py:13
  94.9 4.6 %collective-permute-start.3 = (f32[1]{0:T(128)}, f32[1]{0:T(128)}, u32[]{:S(2)}, u32[]{:S(2)}) collective-permute-start(f32[1]{0:T(128)} %get-tuple-element.29), channel_id=1, source_target_pairs={{1,0},{2,1},{3,2},{4,3},{5,4},{6,5},{7,6},{8,7},{9,8},{10,9},{11,1... | collective-permute-start | bytes 20 | tf_op jit(solution)/shard_map/ppermute | solution.py:13
  102.1 3.0 %copy-start.9 = (f32[4096]{0:T(1024)}, f32[4096]{0:T(1024)S(1)}, u32[]{:S(2)}) copy-start(f32[4096]{0:T(1024)S(1)} %get-tuple-element.21) | copy-start | bytes 49156
  102.1 2.9 %copy-start.12 = (f32[4096]{0:T(1024)}, f32[4096]{0:T(1024)S(1)}, u32[]{:S(2)}) copy-start(f32[4096]{0:T(1024)S(1)} %get-tuple-element.20) | copy-start | bytes 49156
  154.7 28.8 %copy-start.6 = (f32[4096]{0:T(1024)S(1)}, f32[4096]{0:T(1024)}, u32[]{:S(2)}) copy-start(f32[4096]{0:T(1024)} %param.10) | copy-start | bytes 49156
  154.7 28.8 %copy-start.7 = (f32[4096]{0:T(1024)S(1)}, f32[4096]{0:T(1024)}, u32[]{:S(2)}) copy-start(f32[4096]{0:T(1024)} %param.11) | copy-start | bytes 49156
  175.6 9.8 %copy-start.10 = (f32[4096]{0:T(1024)S(1)}, f32[4096]{0:T(1024)}, u32[]{:S(2)}) copy-start(f32[4096]{0:T(1024)} %copy-done.9) | copy-start | bytes 49156
  175.6 9.9 %copy-start.13 = (f32[4096]{0:T(1024)S(1)}, f32[4096]{0:T(1024)}, u32[]{:S(2)}) copy-start(f32[4096]{0:T(1024)} %copy-done.12) | copy-start | bytes 49156
  178.3 3.1 %collective-permute-start.4 = (f32[1]{0:T(128)}, f32[1]{0:T(128)}, u32[]{:S(2)}, u32[]{:S(2)}) collective-permute-start(f32[1]{0:T(128)} %get-tuple-element.26), channel_id=1, source_target_pairs={{0,1},{1,2},{2,3},{3,4},{4,5},{5,6},{6,7},{7,8},{8,9},{9,10},{10,1... | collective-permute-start | bytes 20 | tf_op jit(solution)/shard_map/ppermute | solution.py:13
  180.1 3.4 %collective-permute-start.5 = (f32[1]{0:T(128)}, f32[1]{0:T(128)}, u32[]{:S(2)}, u32[]{:S(2)}) collective-permute-start(f32[1]{0:T(128)} %get-tuple-element.27), channel_id=1, source_target_pairs={{1,0},{2,1},{3,2},{4,3},{5,4},{6,5},{7,6},{8,7},{9,8},{10,9},{11,1... | collective-permute-start | bytes 20 | tf_op jit(solution)/shard_map/ppermute | solution.py:13
  185.4 3.0 %copy-start.14 = (f32[4096]{0:T(1024)}, f32[4096]{0:T(1024)S(1)}, u32[]{:S(2)}) copy-start(f32[4096]{0:T(1024)S(1)} %get-tuple-element.17) | copy-start | bytes 49156
  187.0 69.8 %copy-start.8 = (f32[4096]{0:T(1024)S(1)}, f32[4096]{0:T(1024)}, u32[]{:S(2)}) copy-start(f32[4096]{0:T(1024)} %get-tuple-element.22) | copy-start | bytes 49156
  187.0 69.8 %copy-start.11 = (f32[4096]{0:T(1024)S(1)}, f32[4096]{0:T(1024)}, u32[]{:S(2)}) copy-start(f32[4096]{0:T(1024)} %get-tuple-element.18) | copy-start | bytes 49156
